TPU v7x, 128 devices: a whole 4x4x4 slice. The times are simulated.
128 devices in a mesh: row: 16 (over y_lo, z, core), col: 8 (over x, y_hi).
Axes of the slice: x: 4, y: 4 (y_hi: 2, y_lo: 2; y = y_hi * 2 + y_lo), z: 4, core: 2. Of those that a mesh axis runs over, the one named last changes fastest.
Arguments:
- ladder_ints: float32 [19712, 19712], P('row', 'col'), may hold values from -0.0390625 to 0.0390625
- amplitudes: float32 [19712, 2048], P('row', 'col'), may hold values from -6 to 6
- phase_map: int32 [16], replicated, may hold values from 0 to 15, each once
Outputs:
- ladder_term: float32 [19712, 2048], P('row', 'col')
Inputs may be any that keep to these rules, and one draw needn't show every extreme that they name: `phase_map`: each phase appears once.
All inputs are finite; a program needn't handle non-finite values.
Results may differ from a plain program's by a relative error of at most 0.000078.
Values sent between devices are 32-bit elements; how exact they have to be, the bound alone decides.
A program may use at most 320 MiB of HBM per device.

v0:
```python
import jax
import jax.numpy as jnp
from jax import lax
from jax.sharding import PartitionSpec as P


def per_device(ladder_ints, amplitudes, phase_map):
    phases = lax.axis_size("row")
    spread = lax.all_to_all(amplitudes, "col", split_axis=0, concat_axis=1, tiled=True)
    rows_each = spread.shape[0]
    total_ij = spread.shape[1]
    inverse = jnp.zeros((phases,), jnp.int32).at[phase_map].set(jnp.arange(phases, dtype=jnp.int32))
    shaped = spread.reshape(rows_each, phases, total_ij // phases)
    arrived = lax.all_to_all(shaped, "row", split_axis=1, concat_axis=1, tiled=True)
    ordered = jnp.take(arrived, inverse, axis=1).reshape(rows_each * phases, total_ij // phases)
    partial_value = jnp.dot(
        ladder_ints,
        lax.all_gather(ordered, "row", axis=1, tiled=True),
        precision=lax.Precision.HIGHEST,
        preferred_element_type=jnp.float32,
    )
    return lax.psum_scatter(partial_value, "col", scatter_dimension=1, tiled=True)


def solution(mesh):
    in_specs = (P("row", "col"), P("row", "col"), P())
    out_specs = P("row", "col")
    return jax.shard_map(
        per_device, mesh=mesh, in_specs=in_specs, out_specs=out_specs, check_vma=False
    )
```

profile of v0, /device:TPU:1, one launch (start us, length us, event | category | flops | bytes accessed | tf_op | source)
XLA Modules:
  0.0 399.3 jit_solution(7018368690503459611)
XLA Ops:
  6.5 1.4 all_to_all.15
  8.0 25.4 %all_to_all.21 = f32[8,154,256]{2,1,0:T(8,128)S(1)} all-to-all(f32[8,154,256]{2,1,0:T(8,128)S(1)} %all_to_all.15), channel_id=1, replica_groups=mesh['row'=16,'col'=8] {'col'}, dimensions={0} | all-to-all | bytes 2523136 | tf_op jit(solution)/shard_map/all_to_all | solution.py:9
  33.4 0.7 copy.6
  34.2 0.1 reshape.15
  34.2 1.5 copy.7
  35.7 0.0 copy-start
  35.7 8.0 %all-to-all-start.1 = ((f32[154,16,128]{2,0,1:T(8,128)}), f32[154,16,128]{2,0,1:T(8,128)S(1)}, u32[]{:S(2)}, u32[]{:S(2)}) async-start(f32[154,16,128]{2,0,1:T(8,128)} %copy.7), calls=%async_computation.1 | async-start | bytes 2621440 | tf_op jit(solution)/shard_map/all_to_all | solution.py:14
  43.7 0.0 all-gather.2.cloned.1.call-start
  43.8 0.0 copy-done
  43.8 0.6 scatter_custom_fusion
  44.5 0.1 broadcast_in_dim.21
  44.6 17.6 %all-to-all-done.1 = f32[154,16,128]{2,0,1:T(8,128)S(1)} async-done(((f32[154,16,128]{2,0,1:T(8,128)}), f32[154,16,128]{2,0,1:T(8,128)S(1)}, u32[]{:S(2)}, u32[]{:S(2)}) %all-to-all-start.1) | async-done | bytes 1261600 | tf_op jit(solution)/shard_map/all_to_all | solution.py:14
  62.2 0.6 gather_fusion
  62.9 0.7 copy.8
  63.6 2.1 bitcast_select_fusion
  65.8 0.0 all-gather.2.cloned.1.call-update
  65.8 0.2 reduce-scatter.2.cloned.1.call-start
  66.0 111.9 %all-gather.2.cloned.1.call-done = f32[2464,2048]{1,0:T(8,128)} async-done(((f32[2464,128]{1,0:T(8,128)}), f32[2464,2048]{1,0:T(8,128)}) %all-gather.2.cloned.1.call-update) | async-done | bytes 20185104 | tf_op jit(solution)/shard_map/all_gather | solution.py:18
  177.9 88.6 %convolution_bitcast_fusion = f32[1232,2048]{1,0:T(8,128)} fusion(f32[2464,2048]{1,0:T(8,128)} %all-gather.2.cloned.1.call-done, f32[1232,2464]{1,0:T(8,128)} %param.3), kind=kOutput, calls=%fused_computation.2 | convolution fusion | flops 74604085248 | bytes 42420224 | tf_op jit(solution)/shard_map/dot_general | solution.py:16
  266.5 0.0 reduce-scatter.2.cloned.1.call-update
  266.5 125.9 %reduce-scatter.2.cloned.1.call-done = f32[1232,256]{1,0:T(8,128)} async-done(((f32[1232,2048]{1,0:T(8,128)}), f32[1232,256]{1,0:T(8,128)}) %reduce-scatter.2.cloned.1.call-update) | async-done | bytes 1261584 | tf_op jit(solution)/shard_map/reduce_scatter | solution.py:22
  (6 shorter events, 0.0 us)
Async XLA Ops:
  35.7 8.1 %copy-start = (s32[16]{0:T(128)S(1)}, s32[16]{0:T(128)}, u32[]{:S(2)}) copy-start(s32[16]{0:T(128)} %param.5) | copy-start | bytes 196
  35.7 26.5 %all-to-all-start.1 = ((f32[154,16,128]{2,0,1:T(8,128)}), f32[154,16,128]{2,0,1:T(8,128)S(1)}, u32[]{:S(2)}, u32[]{:S(2)}) async-start(f32[154,16,128]{2,0,1:T(8,128)} %copy.7), calls=%async_computation.1 | async-start | bytes 2621440 | tf_op jit(solution)/shard_map/all_to_all | solution.py:14
  43.7 134.2 %all-gather.2.cloned.1.call-start = ((), (), s32[]{:S(2)}) async-start(), calls=%async_computation.3 | async-start | bytes 21446656 | tf_op jit(solution)/shard_map/all_gather | solution.py:18
  65.8 326.6 %reduce-scatter.2.cloned.1.call-start = ((), (), s32[]{:S(2)}) async-start(), calls=%async_computation.4 | async-start | bytes 11354112 | tf_op jit(solution)/shard_map/reduce_scatter | solution.py:22
Sparse Core Ops, SparseCore 0:
  65.9 111.9 all-gather.1
  266.7 125.7 reduce-scatter.1
where the time goes:
time: 400 us; the launch traced here: 399 us
  waiting for transfers between devices  256 us (64%)
  matrix products  88.6 us (22%)
  blocking collectives  25.4 us (6%)
  between operations  13.5 us (3%)
  starting transfers between devices  8.28 us (2%)
  local copies, waits for them, and re-layouts  5.83 us (1%)
    reduce_scatter x1, waiting for transfers between devices, per_device(): lax.psum_scatter(partial_value, 'col', scatter_dimension=1, tiled=True)  126 us
    all_gather x1, waiting for transfers between devices, per_device(): lax.all_gather(ordered, 'row', axis=1, tiled=True)  112 us
    dot_general x1, matrix products, per_device(): jnp.dot(ladder_ints, lax.all_gather(ordered, 'row', axis=1, tiled=True),...  88.6 us
    all_to_all x1, blocking collectives, per_device(): lax.all_to_all(amplitudes, 'col', split_axis=0, concat_axis=1, tiled=True)  25.4 us
    all_to_all x1, waiting for transfers between devices, per_device(): lax.all_to_all(shaped, 'row', split_axis=1, concat_axis=1, tiled=True)  17.6 us
    all_to_all x1, starting transfers between devices, per_device(): lax.all_to_all(shaped, 'row', split_axis=1, concat_axis=1, tiled=True)  8.02 us
  transfers between devices with their start and end apart: 3, of which 3 were waited for; matrix products, arithmetic and copies ran while one was open for 0% of the time, Pallas kernels for 0%

commit v1 on v0

v1 whole, which is shorter than its diff:
```python
import jax
import jax.numpy as jnp
from jax import lax
from jax.experimental import pallas as pl
from jax.experimental.pallas import tpu as pltpu
from jax.sharding import PartitionSpec as P

UNITS = ((2, 1), (2, 0), (1, 1), (3, 1), (0, 1), (1, 0), (3, 0), (0, 0))
N_UNITS = 8
KPAD = 160
KTOT = 16 * KPAD
NB = 256
MESH = pl.DeviceIdType.MESH


def kernel(rows, depth, v_hbm, a_ref, perm_ref, out_hbm,
           T, Vh, Vl, Th, Tl, Pt, RA, RD, RY, Vs,
           arecv, asend, yrecv, ysend, zrecv, zsend, frecv, fsend, drecv, dsend,
           hrecv, hsend, xrecv, xsend, rysem, vsem, osem):
    r = lax.axis_index("row")
    c = lax.axis_index("col")
    x = c // 2
    yh = c % 2
    yl = r // 8
    z = (r // 2) % 4
    core = r % 2
    half = rows // 2

    def col_of(dx, other):
        return ((x + dx) % 4) * 2 + (yh + other) % 2

    def row_of(other):
        return ((yl + other) % 2) * 8 + z * 2 + core

    row_y = ((yl + 1) % 2) * 8 + z * 2 + core
    row_zp = yl * 8 + ((z + 1) % 4) * 2 + core
    row_zm = yl * 8 + ((z + 3) % 4) * 2 + core
    row_c = yl * 8 + z * 2 + (core + 1) % 2
    zm = (z + 3) % 4
    zp = (z + 1) % 4
    z2 = (z + 2) % 4

    def remote(src, dst, ssem, rsem, row, col):
        return pltpu.make_async_remote_copy(
            src_ref=src, dst_ref=dst, send_sem=ssem, recv_sem=rsem,
            device_id={"row": row, "col": col}, device_id_type=MESH)

    barrier = pltpu.get_barrier_semaphore()
    peers = [(row_of(o), col_of(dx, o)) for dx, o in UNITS if (dx, o) != (0, 0)]
    peers += [(row_y, c), (row_zp, c), (row_zm, c), (row_c, c), (r, col_of(0, 1))]
    for pr, pc in peers:
        pl.semaphore_signal(barrier, inc=1, device_id={"row": pr, "col": pc}, device_id_type=MESH)

    RT = Vs.shape[1]
    n_rt = rows // RT

    def v_copy(i, slot):
        return pltpu.make_async_copy(v_hbm.at[pl.ds(i * RT, RT), :], Vs.at[slot], vsem.at[slot])

    v_copy(0, 0).start()
    pl.semaphore_wait(barrier, len(peers))

    def slot_src(u):
        return core * 8 + z * 2 + (yl + UNITS[u][1]) % 2

    def a2a(u):
        dx, o = UNITS[u]
        dcol = col_of(4 - dx, o)
        return remote(a_ref.at[dcol], T.at[u, core * 8 + z * 2 + yl], asend.at[u], arecv.at[u], row_of(o), dcol)

    def a2a_in(u):
        return remote(a_ref.at[0], T.at[u, slot_src(u)], asend.at[u], arecv.at[u], r, c)

    def ycopy(u):
        s = slot_src(u)
        return remote(T.at[u, s], T.at[u, s], ysend.at[u], yrecv.at[u], row_y, c)

    def pair(u, zz):
        return T.at[u, pl.ds(core * 8 + zz * 2, 2)]

    def zcopy(u, way):
        return remote(pair(u, z), pair(u, z), zsend.at[u, way], zrecv.at[u, way], (row_zp, row_zm)[way], c)

    def fcopy(u, way):
        s = core * 8 + (zm, zp)[way] * 2 + way
        return remote(T.at[u, s], T.at[u, s], fsend.at[u, way], frecv.at[u, way], (row_zp, row_zm)[way], c)

    def dcopy(u, i):
        p = pair(u, (z, zm, zp, z2)[i])
        return remote(p, p, dsend.at[u, i], drecv.at[u, i], row_c, c)

    def S1(u):
        if u < N_UNITS - 1:
            a2a_in(u).wait_recv()
        ycopy(u).start()

    def S2(u):
        ycopy(u).wait_recv()
        zcopy(u, 0).start()
        zcopy(u, 1).start()
        dcopy(u, 0).start()

    def S3(u):
        for way in (0, 1):
            zcopy(u, way).wait_recv()
            fcopy(u, way).start()
        dcopy(u, 1).start()
        dcopy(u, 2).start()

    def S4(u):
        fcopy(u, 0).wait_recv()
        fcopy(u, 1).wait_recv()
        dcopy(u, 3).start()

    def S5(u):
        for i in range(4):
            dcopy(u, i).wait_recv()

    def vprep(lo, hi):
        @pl.loop(lo, hi)
        def _(i):
            slot = i % 2

            @pl.when(i + 1 < n_rt)
            def _():
                v_copy(i + 1, (i + 1) % 2).start()

            v_copy(i, slot).wait()
            rs = pl.ds(pl.multiple_of(i * RT, RT), RT)
            for j in range(KTOT // 256):
                w = min(256, depth - j * 256)
                v = Vs[slot, :, j * 256:j * 256 + w]
                h = v.astype(jnp.bfloat16)
                l = (v - h.astype(jnp.float32)).astype(jnp.bfloat16)
                p = perm_ref[0:w, :]
                Vh[rs, j * 256:(j + 1) * 256] = jnp.dot(h, p, preferred_element_type=jnp.float32).astype(jnp.bfloat16)
                Vl[rs, j * 256:(j + 1) * 256] = jnp.dot(l, p, preferred_element_type=jnp.float32).astype(jnp.bfloat16)

    def prep(u):
        @pl.loop(0, KPAD // 8)
        def _(kb):
            t = T[u, :, pl.ds(pl.multiple_of(kb * 8, 8), 8), :].reshape(128, NB)
            h = t.astype(jnp.bfloat16)
            ks = pl.ds(pl.multiple_of(kb * 128, 128), 128)
            Th[ks, :] = h
            Tl[ks, :] = (t - h.astype(jnp.float32)).astype(jnp.bfloat16)

    MT = 176

    def mm(u, lo, hi):
        @pl.loop(lo, hi)
        def _(i):
            rs = pl.ds(pl.multiple_of(i * MT, MT), MT)
            vh = Vh[rs, :]
            acc = jnp.dot(vh, Tl[...], preferred_element_type=jnp.float32)
            acc += jnp.dot(Vl[rs, :], Th[...], preferred_element_type=jnp.float32)
            acc += jnp.dot(vh, Th[...], preferred_element_type=jnp.float32)
            Pt[u, rs, :] = acc

    def add(dst, srcs, n):
        @pl.loop(0, n // 56)
        def _(i):
            rs = pl.ds(pl.multiple_of(i * 56, 8), 56)
            t = dst[rs, :]
            for s in srcs:
                t = t + s[rs, :]
            dst[rs, :] = t

    def half_copy(h, way):
        u = (0, 1)[1 - h]
        return remote(Pt.at[u, pl.ds(way * half, half)], RA.at[h * 2 + way],
                      hsend.at[h * 2 + way], hrecv.at[h * 2 + way], r, col_of((1, 3)[way], 0))

    def full_copy(h, way):
        u = UNITS.index(((1, 3)[way], h))
        return remote(Pt.at[u], RD.at[h * 2 + way], xsend.at[h * 2 + way], xrecv.at[h * 2 + way],
                      r, col_of((1, 3)[way], 0))

    def last_copy():
        return remote(Pt.at[UNITS.index((0, 1))], RY, rysem.at[0], rysem.at[1], r, col_of(0, 1))

    def reduce_step(u):
        dx, h = UNITS[u]
        if dx == 2:
            half_copy(h, 0).start()
            half_copy(h, 1).start()
        elif dx in (1, 3):
            way = 0 if dx == 1 else 1
            half_copy(h, way).wait_recv()
            add(Pt.at[u, pl.ds(way * half, half)], [RA.at[h * 2 + way]], half)
            full_copy(h, way).start()

    def finish(h):
        u = UNITS.index((0, h))
        full_copy(h, 0).wait_recv()
        full_copy(h, 1).wait_recv()
        srcs = [RD.at[h * 2], RD.at[h * 2 + 1]]
        if h == 0:
            last_copy().wait_recv()
            srcs.append(RY)
        add(Pt.at[u], srcs, rows)
        if h == 1:
            last_copy().start()

    for u in range(N_UNITS - 1):
        a2a(u).start()
    T[N_UNITS - 1, core * 8 + z * 2 + yl] = a_ref[c]

    vprep(0, 2)
    S1(0)
    S1(1)
    vprep(2, 4)
    S2(0)
    S1(2)
    vprep(4, 5)
    S2(1)
    S1(3)
    vprep(5, 6)
    S3(0)
    vprep(6, 7)
    S2(2)
    S1(4)
    S3(1)
    S4(0)
    for u in range(N_UNITS):
        S5(u)
        prep(u)
        if u + 5 < N_UNITS:
            S1(u + 5)
        if u + 3 < N_UNITS:
            S2(u + 3)
        mm(u, 0, 4)
        if u + 2 < N_UNITS:
            S3(u + 2)
        mm(u, 4, 7)
        if u + 1 < N_UNITS:
            S4(u + 1)
        reduce_step(u)
        if UNITS[u] == (1, 0):
            finish(1)
    finish(0)
    o = pltpu.make_async_copy(Pt.at[N_UNITS - 1], out_hbm, osem)
    o.start()
    o.wait()
    for u in range(N_UNITS):
        if u < N_UNITS - 1:
            a2a(u).wait_send()
        ycopy(u).wait_send()
        for way in (0, 1):
            zcopy(u, way).wait_send()
            fcopy(u, way).wait_send()
        for i in range(4):
            dcopy(u, i).wait_send()
    for h in (0, 1):
        for way in (0, 1):
            half_copy(h, way).wait_send()
            full_copy(h, way).wait_send()
    last_copy().wait_send()


def per_device(ladder_ints, amplitudes, phase_map):
    rows, depth = ladder_ints.shape
    kb = depth // 16
    a = jnp.pad(amplitudes.reshape(8, kb, NB), ((0, 0), (0, KPAD - kb), (0, 0)))
    slot_phase = phase_map.reshape(2, 4, 2).transpose(2, 1, 0).reshape(16)
    src = jnp.arange(256)
    dst = jnp.arange(256)
    want = (dst // 128) * 128 + (dst % 8) * 16 + jnp.repeat(jnp.tile(slot_phase, 2), 8)
    perm = (src[:, None] == want[None, :]).astype(jnp.bfloat16)
    f32, bf16 = jnp.float32, jnp.bfloat16
    dma = pltpu.SemaphoreType.DMA
    import functools
    return pl.pallas_call(
        functools.partial(kernel, rows, depth),
        out_shape=jax.ShapeDtypeStruct((rows, NB), f32),
        in_specs=[pl.BlockSpec(memory_space=pl.ANY), pl.BlockSpec(memory_space=pltpu.VMEM),
                  pl.BlockSpec(memory_space=pltpu.VMEM)],
        out_specs=pl.BlockSpec(memory_space=pl.ANY),
        scratch_shapes=[
            pltpu.VMEM((N_UNITS, 16, KPAD, NB), f32),
            pltpu.VMEM((rows, KTOT), bf16),
            pltpu.VMEM((rows, KTOT), bf16),
            pltpu.VMEM((KTOT, NB), bf16),
            pltpu.VMEM((KTOT, NB), bf16),
            pltpu.VMEM((N_UNITS, rows, NB), f32),
            pltpu.VMEM((4, rows // 2, NB), f32),
            pltpu.VMEM((4, rows, NB), f32),
            pltpu.VMEM((rows, NB), f32),
            pltpu.VMEM((2, 176, depth), f32),
            dma((8,)), dma((8,)), dma((8,)), dma((8,)), dma((8, 2)), dma((8, 2)), dma((8, 2)), dma((8, 2)),
            dma((8, 4)), dma((8, 4)), dma((4,)), dma((4,)), dma((4,)), dma((4,)), dma((2,)), dma((2,)), dma,
        ],
        compiler_params=pltpu.CompilerParams(
            collective_id=0, has_side_effects=True, vmem_limit_bytes=67043328),
        name="ladder",
    )(ladder_ints, a, perm)


def solution(mesh):
    in_specs = (P("row", "col"), P("row", "col"), P())
    out_specs = P("row", "col")
    return jax.shard_map(
        per_device, mesh=mesh, in_specs=in_specs, out_specs=out_specs, check_vma=False
    )
```

time: 400 us -> 154 us (0.39)
  waiting for transfers between devices: 256 us -> 0 us
  Pallas kernels: 0 us -> 145 us
  matrix products: 88.6 us -> 0 us
  blocking collectives: 25.4 us -> 0 us
  between operations: 13.5 us -> 0.03 us
  starting transfers between devices: 8.28 us -> 0 us
    pallas_call x0 -> x1, Pallas kernels: none -> 145 us  [per_device(): pl.pallas_call(functools.partial(kernel, rows, depth), out_shape=jax.Shap...]
    reduce_scatter x1 -> x0, waiting for transfers between devices: 126 us -> none  [per_device(): lax.psum_scatter(partial_value, 'col', scatter_dimension=1, tiled=True)]
    all_gather x1 -> x0, waiting for transfers between devices: 112 us -> none  [per_device(): lax.all_gather(ordered, 'row', axis=1, tiled=True)]
    dot_general x1 -> x0, matrix products: 88.6 us -> none  [per_device(): jnp.dot(ladder_ints, lax.all_gather(ordered, 'row', axis=1, tiled=True),...]
    all_to_all x1 -> x0, blocking collectives: 25.4 us -> none  [per_device(): lax.all_to_all(amplitudes, 'col', split_axis=0, concat_axis=1, tiled=True)]
    all_to_all x1 -> x0, waiting for transfers between devices: 17.6 us -> none  [per_device(): lax.all_to_all(shaped, 'row', split_axis=1, concat_axis=1, tiled=True)]
    all_to_all x1 -> x0, starting transfers between devices: 8.02 us -> none  [per_device(): lax.all_to_all(shaped, 'row', split_axis=1, concat_axis=1, tiled=True)]
  transfers between devices with their start and end apart: 3 -> 0, of which waited for: 3 -> 0; matrix products, arithmetic and copies ran while one was open for 0% -> 0% of each run, Pallas kernels for 0% -> 0%
where the time goes in v1:
time: 154 us; the launch traced here: 151 us
  Pallas kernels  145 us (94%)
  local copies, waits for them, and re-layouts  5.63 us (4%)
    pallas_call x1, Pallas kernels, per_device(): pl.pallas_call(functools.partial(kernel, rows, depth), out_shape=jax.Shap...  145 us

profile of v1, /device:TPU:1, one launch (start us, length us, event | category | flops | bytes accessed | tf_op | source)
XLA Modules:
  0.0 151.0 jit_solution(12463348132528873699)
XLA Ops:
  0.0 1.4 reshape.38
  1.4 0.0 copy-start
  1.5 1.2 pad.4.a_ref
  2.7 0.0 copy-done
  2.7 0.1 reshape.39
  2.8 0.1 copy.5
  2.9 0.1 tile.10
  3.0 0.1 tile.12
  3.1 0.1 broadcast_in_dim.2
  3.1 0.1 reshape.40
  3.2 0.7 fusion.perm_ref
  3.9 144.7 %ladder.1 = f32[1232,256]{1,0:T(8,128)} custom-call(f32[1232,2464]{1,0:T(8,128)} %v_hbm.1, f32[8,160,256]{2,1,0:T(8,128)} %pad.4.a_ref, bf16[256,256]{1,0:T(8,128)(2,1)} %fusion.perm_ref), custom_call_target="tpu_custom_call" | custom-call | tf_op jit(solution)/shard_map/ladder/pallas_call | solution.py:273
  148.6 2.4 %copy.7 = f32[1232,256]{1,0:T(8,128)} copy(f32[1232,256]{1,0:T(8,128)} %ladder.1) | data formatting | bytes 2523136
  (2 shorter events, 0.0 us)
Async XLA Ops:
  1.4 1.2 copy-start

commit v2 on v0

v2 whole, which is shorter than its diff:
```python
import functools

import jax
import jax.numpy as jnp
from jax import lax
from jax.experimental import pallas as pl
from jax.experimental.pallas import tpu as pltpu
from jax.sharding import PartitionSpec as P

UNITS = ((2, 1), (2, 0), (1, 1), (3, 1), (1, 0), (3, 0), (0, 1), (0, 0))
N_UNITS = 8
KPAD = 160
KTOT = 16 * KPAD
NB = 256
RT = 176
CUT = (3, 4)
MESH = pl.DeviceIdType.MESH


def kernel(rows, depth, v_hbm, amp, phase, out_s, out_y,
           apad, perm, T, Vh, Vl, Th, Tl, Pt, RA, RD, RY, Vs,
           arecv, asend, yrecv, ysend, zrecv, zsend, frecv, fsend, drecv, dsend,
           hrecv, hsend, xrecv, xsend, lrecv, lsend, vsem, osem):
    r = lax.axis_index("row")
    c = lax.axis_index("col")
    x = c // 2
    yh = c % 2
    yl = r // 8
    z = (r // 2) % 4
    core = r % 2
    kb = depth // 16
    n_rt = rows // RT

    def col_of(dx, other):
        return ((x + dx) % 4) * 2 + (yh + other) % 2

    def row_of(other):
        return ((yl + other) % 2) * 8 + z * 2 + core

    row_y = row_of(1)
    zs = (z, (z + 3) % 4, (z + 1) % 4, (z + 2) % 4)
    row_zp = yl * 8 + zs[2] * 2 + core
    row_zm = yl * 8 + zs[1] * 2 + core
    row_z = (row_zp, row_zm)
    row_c = yl * 8 + z * 2 + (core + 1) % 2

    def remote(src, dst, ssem, rsem, row, col):
        return pltpu.make_async_remote_copy(
            src_ref=src, dst_ref=dst, send_sem=ssem, recv_sem=rsem,
            device_id={"row": row, "col": col}, device_id_type=MESH)

    barrier = pltpu.get_barrier_semaphore()
    peers = [(row_of(o), col_of(dx, o)) for dx, o in UNITS if (dx, o) != (0, 0)]
    peers += [(row_y, c), (row_zp, c), (row_zm, c), (row_c, c), (r, col_of(0, 1))]
    for pr, pc in peers:
        pl.semaphore_signal(barrier, inc=1, device_id={"row": pr, "col": pc}, device_id_type=MESH)

    def v_copy(i, slot):
        return pltpu.make_async_copy(v_hbm.at[pl.ds(i * RT, RT), :], Vs.at[slot], vsem.at[slot])

    def own(u):
        return (yl + UNITS[u][1]) % 2

    def slot(zz, ys):
        return core * 8 + zz * 2 + ys

    def a2a(u):
        dx, o = UNITS[u]
        dcol = col_of(4 - dx, o)
        return remote(apad.at[dcol], T.at[u, slot(z, yl)], asend.at[u], arecv.at[u], row_of(o), dcol)

    def a2a_in(u):
        return remote(apad.at[0], T.at[u, slot(z, own(u))], asend.at[u], arecv.at[u], r, c)

    def ycopy(u, i):
        ref = T.at[u, slot(zs[3 * i], own(u))]
        return remote(ref, ref, ysend.at[u, i], yrecv.at[u, i], row_y, c)

    def ycopy_in(u, i):
        ref = T.at[u, slot(zs[3 * i], 1 - own(u))]
        return remote(ref, ref, ysend.at[u, i], yrecv.at[u, i], row_y, c)

    def zcopy(u, way, k):
        ref = T.at[u, slot(z, (own(u) + k) % 2)]
        return remote(ref, ref, zsend.at[u, way * 2 + k], zrecv.at[u, way * 2 + k], row_z[way], c)

    def zcopy_in(u, way, k):
        ref = T.at[u, slot(zs[1 + way], (own(u) + k) % 2)]
        return remote(ref, ref, zsend.at[u, way * 2 + k], zrecv.at[u, way * 2 + k], row_z[way], c)

    hk = KPAD // 2

    def fcopy(u, way):
        ref = T.at[u, slot(zs[1 + way], own(u)), pl.ds(way * hk, hk)]
        return remote(ref, ref, fsend.at[u, way], frecv.at[u, way], row_z[way], c)

    def fcopy_in(u, way):
        ref = T.at[u, slot(zs[3], own(u)), pl.ds(way * hk, hk)]
        return remote(ref, ref, fsend.at[u, way], frecv.at[u, way], row_z[way], c)

    def dcopy(u, i):
        ref = T.at[u, pl.ds(core * 8 + zs[i] * 2, 2)]
        return remote(ref, ref, dsend.at[u, i], drecv.at[u, i], row_c, c)

    def dcopy_in(u, i):
        ref = T.at[u, pl.ds((1 - core) * 8 + zs[i] * 2, 2)]
        return remote(ref, ref, dsend.at[u, i], drecv.at[u, i], row_c, c)

    def E1(u):
        if UNITS[u] != (0, 0):
            a2a_in(u).wait_recv()
        zcopy(u, 0, 0).start()
        zcopy(u, 1, 0).start()
        ycopy(u, 0).start()

    def E2(u):
        ycopy_in(u, 0).wait_recv()
        zcopy(u, 0, 1).start()
        zcopy(u, 1, 1).start()
        dcopy(u, 0).start()

    def E3(u):
        for way in (0, 1):
            zcopy_in(u, way, 0).wait_recv()
            fcopy(u, way).start()

    def E4(u):
        fcopy_in(u, 0).wait_recv()
        fcopy_in(u, 1).wait_recv()
        ycopy(u, 1).start()

    def E5(u):
        for way in (0, 1):
            zcopy_in(u, way, 1).wait_recv()
            dcopy(u, 1 + way).start()

    def E6(u):
        ycopy_in(u, 1).wait_recv()
        dcopy(u, 3).start()

    def E7(u):
        for i in range(4):
            dcopy_in(u, i).wait_recv()

    def vprep(lo, hi):
        @pl.loop(lo, hi)
        def _(i):
            s = i % 2

            @pl.when(i + 1 < n_rt)
            def _():
                v_copy(i + 1, (i + 1) % 2).start()

            v_copy(i, s).wait()
            rs = pl.ds(pl.multiple_of(i * RT, RT), RT)
            for j in range(KTOT // 256):
                w = min(256, depth - j * 256)
                v = Vs[s, :, j * 256:j * 256 + w]
                h = v.astype(jnp.bfloat16)
                l = (v - h.astype(jnp.float32)).astype(jnp.bfloat16)
                p = perm[0:w, :]
                Vh[rs, j * 256:(j + 1) * 256] = jnp.dot(h, p, preferred_element_type=jnp.float32).astype(jnp.bfloat16)
                Vl[rs, j * 256:(j + 1) * 256] = jnp.dot(l, p, preferred_element_type=jnp.float32).astype(jnp.bfloat16)

    def aprep():
        for j in range(8):
            apad[j, 0:kb, :] = amp[j * kb:(j + 1) * kb, :]
            apad[j, kb:KPAD, :] = jnp.zeros((KPAD - kb, NB), jnp.float32)

    def permprep():
        lane = lax.broadcasted_iota(jnp.int32, (1, 256), 1)
        want = (lane // 128) * 128 + (lane % 8) * 16
        which = (lane % 128) // 8
        for s in range(16):
            g = (s % 2) * 8 + ((s // 2) % 4) * 2 + s // 8
            want = want + jnp.where(which == s, phase[g], 0)
        rowi = lax.broadcasted_iota(jnp.int32, (256, 256), 0)
        perm[...] = jnp.where(rowi == want, 1.0, 0.0).astype(jnp.bfloat16)

    def prep(u):
        @pl.loop(0, KPAD // 8)
        def _(k):
            t = T[u, :, pl.ds(pl.multiple_of(k * 8, 8), 8), :].reshape(128, NB)
            h = t.astype(jnp.bfloat16)
            ks = pl.ds(pl.multiple_of(k * 128, 128), 128)
            Th[ks, :] = h
            Tl[ks, :] = (t - h.astype(jnp.float32)).astype(jnp.bfloat16)

    def mm(u, lo, hi):
        @pl.loop(lo, hi)
        def _(i):
            rs = pl.ds(pl.multiple_of(i * RT, RT), RT)
            vh = Vh[rs, :]
            acc = jnp.dot(vh, Tl[...], preferred_element_type=jnp.float32)
            acc += jnp.dot(Vl[rs, :], Th[...], preferred_element_type=jnp.float32)
            acc += jnp.dot(vh, Th[...], preferred_element_type=jnp.float32)
            Pt[u, rs, :] = acc

    def add(dst, srcs, lo, n, off=0):
        @pl.loop(0, n // 88)
        def _(i):
            rs = pl.ds(pl.multiple_of(lo + i * 88, 8), 88)
            t = dst[rs, :]
            for s in srcs:
                t = t + s[pl.ds(pl.multiple_of(lo - off + i * 88, 8), 88), :]
            dst[rs, :] = t

    def part(h, k):
        cut = CUT[h] * RT
        return (0, cut) if k == 0 else (cut, rows - cut)

    def half_copy(h, way):
        lo, n = part(h, way)
        return remote(Pt.at[UNITS.index((2, h)), pl.ds(lo, n)], RA.at[h * 2 + way, pl.ds(0, n)],
                      hsend.at[h * 2 + way], hrecv.at[h * 2 + way], r, col_of((1, 3)[way], 0))

    def full_copy(h, way, k):
        lo, n = part(h, k)
        u = UNITS.index(((1, 3)[way], h))
        i = h * 2 + way
        return remote(Pt.at[u, pl.ds(lo, n)], RD.at[i, pl.ds(lo, n)], xsend.at[i, k], xrecv.at[i, k],
                      r, col_of((1, 3)[way], 0))

    def last_copy(k):
        lo, n = part(1, k)
        return remote(Pt.at[UNITS.index((0, 1)), pl.ds(lo, n)], RY.at[pl.ds(lo, n)], lsend.at[k], lrecv.at[k],
                      r, col_of(0, 1))

    def reduce_step(u, k):
        dx, h = UNITS[u]
        if dx == 2:
            half_copy(h, k).start()
        elif dx in (1, 3):
            way = 0 if dx == 1 else 1
            if way == k:
                half_copy(h, way).wait_recv()
                lo, n = part(h, k)
                add(Pt.at[u], [RA.at[h * 2 + way]], lo, n, lo)
            full_copy(h, way, k).start()

    def finish(h, k):
        u = UNITS.index((0, h))
        lo, n = part(h, k)
        full_copy(h, 0, k).wait_recv()
        full_copy(h, 1, k).wait_recv()
        add(Pt.at[u], [RD.at[h * 2], RD.at[h * 2 + 1]], lo, n)
        if h == 1:
            last_copy(k).start()
        else:
            out_copy(k).start()

    def out_copy(k):
        lo, n = part(0, k)
        return pltpu.make_async_copy(Pt.at[UNITS.index((0, 0)), pl.ds(lo, n)], out_s.at[pl.ds(lo, n)], osem.at[k])

    y_copy = pltpu.make_async_copy(RY, out_y, osem.at[2])

    def unit(u):
        E7(u)
        prep(u)
        cut = CUT[UNITS[u][1]]
        mm(u, 0, 2)
        if u + 1 < N_UNITS:
            E4(u + 1)
            E5(u + 1)
        mm(u, 2, cut)
        reduce_step(u, 0)
        if u + 2 < N_UNITS:
            E2(u + 2)
            E3(u + 2)
        if u + 3 < N_UNITS:
            E1(u + 3)
        mm(u, cut, n_rt)
        reduce_step(u, 1)
        if u + 1 < N_UNITS:
            E6(u + 1)

    v_copy(0, 0).start()
    aprep()
    permprep()
    vprep(0, 1)
    pl.semaphore_wait(barrier, len(peers))
    a2a(0).start()
    a2a(1).start()
    T[N_UNITS - 1, slot(z, yl)] = apad[c]
    vprep(1, 3)
    for u in range(2, N_UNITS - 1):
        a2a(u).start()
    E1(0)
    vprep(3, 5)
    E2(0)
    E3(0)
    E1(1)
    vprep(5, 7)
    E5(0)
    E4(0)
    E2(1)
    E3(1)
    E1(2)
    E6(0)
    for u in range(N_UNITS):
        unit(u)
        if UNITS[u] == (0, 1):
            finish(1, 0)
            finish(1, 1)
    last_copy(0).wait_recv()
    last_copy(1).wait_recv()
    y_copy.start()
    finish(0, 0)
    finish(0, 1)
    for u in range(N_UNITS):
        if UNITS[u] != (0, 0):
            a2a(u).wait_send()
        for i in (0, 1):
            ycopy(u, i).wait_send()
            fcopy(u, i).wait_send()
            for k in (0, 1):
                zcopy(u, i, k).wait_send()
        for i in range(4):
            dcopy(u, i).wait_send()
    for k in (0, 1):
        for h in (0, 1):
            half_copy(h, k).wait_send()
            for way in (0, 1):
                full_copy(h, way, k).wait_send()
        last_copy(k).wait_send()
        out_copy(k).wait()
    y_copy.wait()


def per_device(ladder_ints, amplitudes, phase_map):
    rows, depth = ladder_ints.shape
    f32, bf16 = jnp.float32, jnp.bfloat16
    dma = pltpu.SemaphoreType.DMA
    out = jax.ShapeDtypeStruct((rows, NB), f32)
    s, y = pl.pallas_call(
        functools.partial(kernel, rows, depth),
        out_shape=(out, out),
        in_specs=[pl.BlockSpec(memory_space=pl.ANY), pl.BlockSpec(memory_space=pltpu.VMEM),
                  pl.BlockSpec(memory_space=pltpu.SMEM)],
        out_specs=(pl.BlockSpec(memory_space=pl.ANY), pl.BlockSpec(memory_space=pl.ANY)),
        scratch_shapes=[
            pltpu.VMEM((8, KPAD, NB), f32),
            pltpu.VMEM((256, 256), bf16),
            pltpu.VMEM((N_UNITS, 16, KPAD, NB), f32),
            pltpu.VMEM((rows, KTOT), bf16),
            pltpu.VMEM((rows, KTOT), bf16),
            pltpu.VMEM((KTOT, NB), bf16),
            pltpu.VMEM((KTOT, NB), bf16),
            pltpu.VMEM((N_UNITS, rows, NB), f32),
            pltpu.VMEM((4, max(CUT) * RT, NB), f32),
            pltpu.VMEM((4, rows, NB), f32),
            pltpu.VMEM((rows, NB), f32),
            pltpu.VMEM((2, RT, depth), f32),
            dma((8,)), dma((8,)), dma((8, 2)), dma((8, 2)), dma((8, 4)), dma((8, 4)), dma((8, 2)), dma((8, 2)),
            dma((8, 4)), dma((8, 4)), dma((4,)), dma((4,)), dma((4, 2)), dma((4, 2)), dma((2,)), dma((2,)),
            dma((2,)), dma((3,)),
        ],
        compiler_params=pltpu.CompilerParams(
            collective_id=0, has_side_effects=True, vmem_limit_bytes=67043328),
        name="ladder",
    )(ladder_ints, amplitudes, phase_map)
    return s + y


def solution(mesh):
    in_specs = (P("row", "col"), P("row", "col"), P())
    out_specs = P("row", "col")
    return jax.shard_map(
        per_device, mesh=mesh, in_specs=in_specs, out_specs=out_specs, check_vma=False
    )
```

time: 400 us -> 138 us (0.34)
  waiting for transfers between devices: 256 us -> 0 us
  Pallas kernels: 0 us -> 134 us
  matrix products: 88.6 us -> 0 us
  blocking collectives: 25.4 us -> 0 us
  between operations: 13.5 us -> 0.01 us
  starting transfers between devices: 8.28 us -> 0 us
  local copies, waits for them, and re-layouts: 5.83 us -> 0 us
    pallas_call x0 -> x1, Pallas kernels: none -> 134 us  [per_device(): pl.pallas_call(functools.partial(kernel, rows, depth), out_shape=(out, ou...]
    reduce_scatter x1 -> x0, waiting for transfers between devices: 126 us -> none  [per_device(): lax.psum_scatter(partial_value, 'col', scatter_dimension=1, tiled=True)]
    all_gather x1 -> x0, waiting for transfers between devices: 112 us -> none  [per_device(): lax.all_gather(ordered, 'row', axis=1, tiled=True)]
    dot_general x1 -> x0, matrix products: 88.6 us -> none  [per_device(): jnp.dot(ladder_ints, lax.all_gather(ordered, 'row', axis=1, tiled=True),...]
    all_to_all x1 -> x0, blocking collectives: 25.4 us -> none  [per_device(): lax.all_to_all(amplitudes, 'col', split_axis=0, concat_axis=1, tiled=True)]
    all_to_all x1 -> x0, waiting for transfers between devices: 17.6 us -> none  [per_device(): lax.all_to_all(shaped, 'row', split_axis=1, concat_axis=1, tiled=True)]
    all_to_all x1 -> x0, starting transfers between devices: 8.02 us -> none  [per_device(): lax.all_to_all(shaped, 'row', split_axis=1, concat_axis=1, tiled=True)]
  transfers between devices with their start and end apart: 3 -> 0, of which waited for: 3 -> 0; matrix products, arithmetic and copies ran while one was open for 0% -> 0% of each run, Pallas kernels for 0% -> 0%
where the time goes in v2:
time: 138 us; the launch traced here: 137 us
  Pallas kernels  134 us (97%)
  other arithmetic  2.88 us (2%)
    pallas_call x1, Pallas kernels, per_device(): pl.pallas_call(functools.partial(kernel, rows, depth), out_shape=(out, ou...  134 us
    add x1, other arithmetic, per_device(): return s + y  2.88 us

profile of v2, /device:TPU:1, one launch (start us, length us, event | category | flops | bytes accessed | tf_op | source)
XLA Modules:
  0.0 137.4 jit_solution(1463892997407358947)
XLA Ops:
  0.0 134.5 %ladder.1 = (f32[1232,256]{1,0:T(8,128)}, f32[1232,256]{1,0:T(8,128)}) custom-call(f32[1232,2464]{1,0:T(8,128)} %v_hbm.1, f32[1232,256]{1,0:T(8,128)} %amp.1, s32[16]{0:T(128)} %phase.1), custom_call_target="tpu_custom_call" | custom-call | tf_op jit(solution)/shard_map/ladder/pallas_call | solution.py:336
  134.5 2.9 %add.3 = f32[1232,256]{1,0:T(8,128)} add(f32[1232,256]{1,0:T(8,128)} %get-tuple-element.7, f32[1232,256]{1,0:T(8,128)} %get-tuple-element.8) | non-fusion elementwise | flops 315392 | bytes 3784704 | tf_op jit(solution)/shard_map/add | solution.py:363

commit v3 on v0

v3 whole, which is shorter than its diff:
```python
import functools

import jax
import jax.numpy as jnp
from jax import lax
from jax.experimental import pallas as pl
from jax.experimental.pallas import tpu as pltpu
from jax.sharding import PartitionSpec as P

UNITS = (("A", 1, 0), ("A", 0, 0), ("M", 1, 0), ("M", 1, 1), ("M", 0, 0), ("D", 1, 0), ("M", 0, 1), ("D", 0, 0))
N_UNITS = 8
KPAD = 160
KTOT = 16 * KPAD
NB = 256
HB = NB // 2
RT = 176
CUT = 4
STEPS = ((0, 0, KPAD // 2), (0, KPAD // 2, KPAD // 2)) + tuple((u, 0, KPAD) for u in range(1, N_UNITS))
NO_Y2 = (0, 1, 8)
CHUNKS = (((0, RT), (2 * RT, RT), (4 * RT, RT), (6 * RT, RT // 2)),
          ((RT, RT), (3 * RT, RT), (5 * RT, RT), (6 * RT + RT // 2, RT // 2)))
MESH = pl.DeviceIdType.MESH


def kernel(rows, depth, v_hbm, amp_hbm, phase, out,
           amp, apad, perm, T, Vh, Vl, Th, Tl, Pt, RA, RD, RY, Vs,
           arecv, asend, yrecv, ysend, zrecv, zsend, frecv, fsend, drecv, dsend,
           hrecv, hsend, xrecv, xsend, lrecv, lsend, vsem, asem):
    r = lax.axis_index("row")
    c = lax.axis_index("col")
    x = c // 2
    yh = c % 2
    yl = r // 8
    z = (r // 2) % 4
    core = r % 2
    kb = depth // 16
    n_rt = rows // RT

    def col_of(dx, other):
        return ((x + dx) % 4) * 2 + (yh + other) % 2

    def row_of(other):
        return ((yl + other) % 2) * 8 + z * 2 + core

    row_y = row_of(1)
    zs = (z, (z + 3) % 4, (z + 1) % 4, (z + 2) % 4)
    row_zp = yl * 8 + zs[2] * 2 + core
    row_zm = yl * 8 + zs[1] * 2 + core
    row_z = (row_zp, row_zm)
    row_c = yl * 8 + z * 2 + (core + 1) % 2

    def remote(src, dst, ssem, rsem, row, col):
        return pltpu.make_async_remote_copy(
            src_ref=src, dst_ref=dst, send_sem=ssem, recv_sem=rsem,
            device_id={"row": row, "col": col}, device_id_type=MESH)

    barrier = pltpu.get_barrier_semaphore()
    peers = [(row_of(o), col_of(dx, o)) for dx in range(4) for o in (0, 1) if (dx, o) != (0, 0)]
    peers += [(row_y, c), (row_zp, c), (row_zm, c), (row_c, c), (r, col_of(0, 1))]
    for pr, pc in peers:
        pl.semaphore_signal(barrier, inc=1, device_id={"row": pr, "col": pc}, device_id_type=MESH)

    def v_copy(i, slot):
        return pltpu.make_async_copy(v_hbm.at[pl.ds(i * RT, RT), :], Vs.at[slot], vsem.at[slot])

    def own(u):
        return (yl + UNITS[u][1]) % 2

    def slot(zz, ys):
        return core * 8 + zz * 2 + ys

    def piece(g, zz, ys):
        u, lo, n = STEPS[g]
        return T.at[u, slot(zz, ys), pl.ds(lo, n)]

    def a2a_parts(g):
        kind, _, p = UNITS[STEPS[g][0]]
        if kind == "M":
            return ((1, p * HB, HB, 0), (3, p * HB, HB, HB))
        return ((2 if kind == "A" else 0, 0, NB, 0),)

    def a2a(g, i):
        u, lo, n = STEPS[g]
        dx, c0, w, d0 = a2a_parts(g)[i]
        o = UNITS[u][1]
        dcol = col_of(4 - dx, o)
        return remote(apad.at[dcol, pl.ds(lo, n), pl.ds(c0, w)],
                      T.at[u, slot(z, yl), pl.ds(lo, n), pl.ds(d0, w)],
                      asend.at[g, i], arecv.at[g, i], row_of(o), dcol)

    def a2a_in(g, i):
        u, lo, n = STEPS[g]
        _, c0, w, d0 = a2a_parts(g)[i]
        return remote(apad.at[0, pl.ds(lo, n), pl.ds(c0, w)],
                      T.at[u, slot(z, own(u)), pl.ds(lo, n), pl.ds(d0, w)],
                      asend.at[g, i], arecv.at[g, i], r, c)

    def send_out(*gs):
        for g in gs:
            for i in range(len(a2a_parts(g))):
                a2a(g, i).start()

    def ycopy(g, i):
        ref = piece(g, zs[3 * i], own(STEPS[g][0]))
        return remote(ref, ref, ysend.at[g, i], yrecv.at[g, i], row_y, c)

    def ycopy_in(g, i):
        ref = piece(g, zs[3 * i], 1 - own(STEPS[g][0]))
        return remote(ref, ref, ysend.at[g, i], yrecv.at[g, i], row_y, c)

    def zcopy(g, way, k):
        ref = piece(g, z, (own(STEPS[g][0]) + k) % 2)
        return remote(ref, ref, zsend.at[g, way * 2 + k], zrecv.at[g, way * 2 + k], row_z[way], c)

    def zcopy_in(g, way, k):
        ref = piece(g, zs[1 + way], (own(STEPS[g][0]) + k) % 2)
        return remote(ref, ref, zsend.at[g, way * 2 + k], zrecv.at[g, way * 2 + k], row_z[way], c)

    def fpart(g, way, zz, k):
        u, lo, n = STEPS[g]
        return T.at[u, slot(zz, (own(u) + k) % 2), pl.ds(lo + way * (n // 2), n // 2)]

    def fcopy(g, way, k=0):
        ref = fpart(g, way, zs[1 + way], k)
        return remote(ref, ref, fsend.at[g, k * 2 + way], frecv.at[g, k * 2 + way], row_z[way], c)

    def fcopy_in(g, way, k=0):
        ref = fpart(g, way, zs[3], k)
        return remote(ref, ref, fsend.at[g, k * 2 + way], frecv.at[g, k * 2 + way], row_z[way], c)

    def dpair(g, i, k):
        u, lo, n = STEPS[g]
        return T.at[u, pl.ds(k * 8 + zs[i] * 2, 2), pl.ds(lo, n)]

    def dcopy(g, i):
        ref = dpair(g, i, core)
        return remote(ref, ref, dsend.at[g, i], drecv.at[g, i], row_c, c)

    def dcopy_in(g, i):
        ref = dpair(g, i, 1 - core)
        return remote(ref, ref, dsend.at[g, i], drecv.at[g, i], row_c, c)

    def local(g):
        return UNITS[STEPS[g][0]][:2] == ("D", 0)

    def Y0(g):
        if not local(g):
            for i in range(len(a2a_parts(g))):
                a2a_in(g, i).wait_recv()
        ycopy(g, 0).start()

    def Z0(g):
        zcopy(g, 0, 0).start()
        zcopy(g, 1, 0).start()

    def E1(g):
        Y0(g)
        Z0(g)

    def E2(g):
        ycopy_in(g, 0).wait_recv()
        zcopy(g, 0, 1).start()
        zcopy(g, 1, 1).start()
        dcopy(g, 0).start()

    def E3(g):
        for way in (0, 1):
            zcopy_in(g, way, 0).wait_recv()
            fcopy(g, way).start()

    def E4(g):
        fcopy_in(g, 0).wait_recv()
        fcopy_in(g, 1).wait_recv()
        if g not in NO_Y2:
            ycopy(g, 1).start()

    def E5(g):
        for way in (0, 1):
            zcopy_in(g, way, 1).wait_recv()
            if g in NO_Y2:
                fcopy(g, way, 1).start()
            dcopy(g, 1 + way).start()

    def E6(g):
        if g in NO_Y2:
            fcopy_in(g, 0, 1).wait_recv()
            fcopy_in(g, 1, 1).wait_recv()
        else:
            ycopy_in(g, 1).wait_recv()
        dcopy(g, 3).start()

    def E7(g):
        for i in range(4):
            dcopy_in(g, i).wait_recv()

    def vprep(lo, hi):
        @pl.loop(lo, hi)
        def _(i):
            s = i % 2

            @pl.when(i + 1 < n_rt)
            def _():
                v_copy(i + 1, (i + 1) % 2).start()

            v_copy(i, s).wait()
            rs = pl.ds(pl.multiple_of(i * RT, RT), RT)
            for j in range(KTOT // 256):
                w = min(256, depth - j * 256)
                v = Vs[s, :, j * 256:j * 256 + w]
                h = v.astype(jnp.bfloat16)
                l = (v - h.astype(jnp.float32)).astype(jnp.bfloat16)
                p = perm[0:w, :]
                Vh[rs, j * 256:(j + 1) * 256] = jnp.dot(h, p, preferred_element_type=jnp.float32).astype(jnp.bfloat16)
                Vl[rs, j * 256:(j + 1) * 256] = jnp.dot(l, p, preferred_element_type=jnp.float32).astype(jnp.bfloat16)

    def aprep():
        for j in range(8):
            apad[j, 0:kb, :] = amp[j * kb:(j + 1) * kb, :]
            apad[j, kb:KPAD, :] = jnp.zeros((KPAD - kb, NB), jnp.float32)

    def permprep():
        lane = lax.broadcasted_iota(jnp.int32, (1, 256), 1)
        want = (lane // 128) * 128 + (lane % 8) * 16
        which = (lane % 128) // 8
        for s in range(16):
            g = (s % 2) * 8 + ((s // 2) % 4) * 2 + s // 8
            want = want + jnp.where(which == s, phase[g], 0)
        rowi = lax.broadcasted_iota(jnp.int32, (256, 256), 0)
        perm[...] = jnp.where(rowi == want, 1.0, 0.0).astype(jnp.bfloat16)

    def prep(g):
        u, first, n = STEPS[g]

        @pl.loop(first // 8, (first + n) // 8)
        def _(k):
            t = T[u, :, pl.ds(pl.multiple_of(k * 8, 8), 8), :].reshape(128, NB)
            h = t.astype(jnp.bfloat16)
            ks = pl.ds(pl.multiple_of(k * 128, 128), 128)
            Th[ks, :] = h
            Tl[ks, :] = (t - h.astype(jnp.float32)).astype(jnp.bfloat16)

    def mm(u, lo, hi):
        @pl.loop(lo, hi)
        def _(i):
            rs = pl.ds(pl.multiple_of(i * RT, RT), RT)
            vh = Vh[rs, :]
            acc = jnp.dot(vh, Tl[...], preferred_element_type=jnp.float32)
            acc += jnp.dot(Vl[rs, :], Th[...], preferred_element_type=jnp.float32)
            acc += jnp.dot(vh, Th[...], preferred_element_type=jnp.float32)
            Pt[u, rs, :] = acc

    def add_at(dst, src, lo, n, off, d0, s0):
        @pl.loop(0, n // 88)
        def _(i):
            rs = pl.ds(pl.multiple_of(lo + i * 88, 8), 88)
            dst[rs, d0:d0 + HB] += src[pl.ds(pl.multiple_of(lo + off + i * 88, 8), 88), s0:s0 + HB]

    def add(dst, srcs, lo, n, d0):
        @pl.loop(0, n // 88)
        def _(i):
            rs = pl.ds(pl.multiple_of(lo + i * 88, 8), 88)
            t = srcs[-1][rs, d0:d0 + HB]
            for s in srcs[:-1]:
                t = t + s[rs, d0:d0 + HB]
            dst[rs, d0:d0 + HB] = t

    def part(k):
        cut = CUT * RT
        return (0, cut) if k == 0 else (cut, rows - cut)

    def half_copy(h, way, i):
        lo, n = CHUNKS[way][i]
        return remote(Pt.at[UNITS.index(("A", h, 0)), pl.ds(lo, n)], RA.at[h * 2 + way, pl.ds(i * RT, n)],
                      hsend.at[h * 2 + way, i], hrecv.at[h * 2 + way, i], r, col_of((1, 3)[way], 0))

    def full_copy(h, way, p, k):
        lo, n = part(k)
        i = h * 2 + way
        return remote(Pt.at[UNITS.index(("M", h, p)), pl.ds(lo, n), pl.ds(way * HB, HB)],
                      RD.at[i, pl.ds(lo, n), pl.ds(p * HB, HB)],
                      xsend.at[i, p * 2 + k], xrecv.at[i, p * 2 + k], r, col_of((1, 3)[way], 0))

    def last_copy(p):
        cs = pl.ds(p * HB, HB)
        return remote(Pt.at[UNITS.index(("D", 1, 0)), :, cs], RY.at[:, cs], lsend.at[p], lrecv.at[p],
                      r, col_of(0, 1))

    def reduce_step(u, k):
        kind, h, p = UNITS[u]
        if kind == "A":
            for i in ((0,), (1,), (2, 3))[k]:
                half_copy(h, 0, i).start()
                half_copy(h, 1, i).start()
        elif kind == "M" and k > 0:
            for way in (0, 1):
                for i in ((0, 1), (2, 3))[k - 1]:
                    if p == 0:
                        half_copy(h, way, i).wait_recv()
                    lo, n = CHUNKS[way][i]
                    add_at(Pt.at[u], RA.at[h * 2 + way], lo, n, i * RT - lo, way * HB, p * HB)
                full_copy(h, way, p, k - 1).start()

    def finish(h, p):
        u = UNITS.index(("D", h, 0))
        for k in (0, 1):
            for way in (0, 1):
                full_copy(h, way, p, k).wait_recv()
        srcs = [RD.at[h * 2], RD.at[h * 2 + 1]]
        if h == 0:
            last_copy(p).wait_recv()
            srcs.append(RY)
        add(out if h == 0 else Pt.at[u], srcs + [Pt.at[u]], 0, rows, p * HB)
        if h == 1:
            last_copy(p).start()

    def unit(u):
        if u > 0:
            E7(u + 1)
            prep(u + 1)
        mm(u, 0, 2)
        reduce_step(u, 0)
        if u == 0:
            mm(u, 2, CUT)
            reduce_step(u, 1)
        if u + 1 < N_UNITS:
            E4(u + 2)
            E5(u + 2)
        if u == 0:
            E2(3)
            E3(3)
            E1(4)
        else:
            mm(u, 2, CUT)
            reduce_step(u, 1)
        mm(u, CUT, n_rt)
        reduce_step(u, 2)
        if u == 5:
            finish(1, 0)
        if u == 6:
            finish(1, 1)
        if u + 1 < N_UNITS:
            E6(u + 2)
        if u + 3 < N_UNITS:
            E2(u + 4)
            E3(u + 4)
        if u + 4 < N_UNITS:
            E1(u + 5)

    a_copy = pltpu.make_async_copy(amp_hbm, amp, asem)
    a_copy.start()
    v_copy(0, 0).start()
    permprep()
    a_copy.wait()
    aprep()
    pl.semaphore_wait(barrier, len(peers))
    send_out(0, 1)
    vprep(0, 3)
    send_out(2, 3, 4)
    T[N_UNITS - 1, slot(z, yl)] = apad[c]
    vprep(3, 4)
    E1(0)
    send_out(5, 6, 7)
    vprep(4, 5)
    E1(1)
    vprep(5, 6)
    E2(0)
    E3(0)
    E2(1)
    E3(1)
    Y0(2)
    vprep(6, 7)
    E5(0)
    E5(1)
    Z0(2)
    E4(0)
    E4(1)
    E6(0)
    E6(1)
    E2(2)
    Y0(3)
    E7(0)
    prep(0)
    E7(1)
    prep(1)
    E3(2)
    Z0(3)
    for u in range(N_UNITS):
        unit(u)
    finish(0, 0)
    for g in range(len(STEPS)):
        if not local(g):
            for i in range(len(a2a_parts(g))):
                a2a(g, i).wait_send()
        for i in (0, 1):
            if i == 0 or g not in NO_Y2:
                ycopy(g, i).wait_send()
            fcopy(g, i).wait_send()
            if g in NO_Y2:
                fcopy(g, i, 1).wait_send()
            for k in (0, 1):
                zcopy(g, i, k).wait_send()
        for i in range(4):
            dcopy(g, i).wait_send()
    for h in (1, 0):
        for way in (0, 1):
            for i in range(4):
                half_copy(h, way, i).wait_send()
                if h == 1 or i < 2:
                    full_copy(h, way, i // 2, i % 2).wait_send()
    last_copy(0).wait_send()
    finish(0, 1)
    last_copy(1).wait_send()
    for way in (0, 1):
        for k in (0, 1):
            full_copy(0, way, 1, k).wait_send()


def per_device(ladder_ints, amplitudes, phase_map):
    rows, depth = ladder_ints.shape
    f32, bf16 = jnp.float32, jnp.bfloat16
    dma = pltpu.SemaphoreType.DMA
    return pl.pallas_call(
        functools.partial(kernel, rows, depth),
        out_shape=pltpu.VMEM((rows, NB), f32),
        in_specs=[pl.BlockSpec(memory_space=pl.ANY), pl.BlockSpec(memory_space=pl.ANY),
                  pl.BlockSpec(memory_space=pltpu.SMEM)],
        out_specs=pl.BlockSpec(memory_space=pltpu.VMEM),
        scratch_shapes=[
            pltpu.VMEM((rows, NB), f32),
            pltpu.VMEM((8, KPAD, NB), f32),
            pltpu.VMEM((256, 256), bf16),
            pltpu.VMEM((N_UNITS, 16, KPAD, NB), f32),
            pltpu.VMEM((rows, KTOT), bf16),
            pltpu.VMEM((rows, KTOT), bf16),
            pltpu.VMEM((KTOT, NB), bf16),
            pltpu.VMEM((KTOT, NB), bf16),
            pltpu.VMEM((N_UNITS, rows, NB), f32),
            pltpu.VMEM((4, rows // 2, NB), f32),
            pltpu.VMEM((4, rows, NB), f32),
            pltpu.VMEM((rows, NB), f32),
            pltpu.VMEM((2, RT, depth), f32),
            dma((9, 2)), dma((9, 2)), dma((9, 2)), dma((9, 2)), dma((9, 4)), dma((9, 4)), dma((9, 4)), dma((9, 4)),
            dma((9, 4)), dma((9, 4)), dma((4, 4)), dma((4, 4)), dma((4, 4)), dma((4, 4)), dma((2,)), dma((2,)),
            dma((2,)), dma,
        ],
        compiler_params=pltpu.CompilerParams(
            collective_id=0, has_side_effects=True, vmem_limit_bytes=65600000),
        name="ladder",
    )(ladder_ints, amplitudes, phase_map)


def solution(mesh):
    in_specs = (P("row", "col"), P("row", "col"), P())
    out_specs = P("row", "col")
    return jax.shard_map(
        per_device, mesh=mesh, in_specs=in_specs, out_specs=out_specs, check_vma=False
    )
```

time: 400 us -> 128 us (0.32)
  waiting for transfers between devices: 256 us -> 0 us
  Pallas kernels: 0 us -> 127 us
  matrix products: 88.6 us -> 0 us
  blocking collectives: 25.4 us -> 0 us
  between operations: 13.5 us -> 0.01 us
  starting transfers between devices: 8.28 us -> 0 us
  local copies, waits for them, and re-layouts: 5.83 us -> 1.04 us
    pallas_call x0 -> x1, Pallas kernels: none -> 127 us  [per_device(): pl.pallas_call(functools.partial(kernel, rows, depth), out_shape=pltpu.VM...]
    reduce_scatter x1 -> x0, waiting for transfers between devices: 126 us -> none  [per_device(): lax.psum_scatter(partial_value, 'col', scatter_dimension=1, tiled=True)]
    all_gather x1 -> x0, waiting for transfers between devices: 112 us -> none  [per_device(): lax.all_gather(ordered, 'row', axis=1, tiled=True)]
    dot_general x1 -> x0, matrix products: 88.6 us -> none  [per_device(): jnp.dot(ladder_ints, lax.all_gather(ordered, 'row', axis=1, tiled=True),...]
    all_to_all x1 -> x0, blocking collectives: 25.4 us -> none  [per_device(): lax.all_to_all(amplitudes, 'col', split_axis=0, concat_axis=1, tiled=True)]
    all_to_all x1 -> x0, waiting for transfers between devices: 17.6 us -> none  [per_device(): lax.all_to_all(shaped, 'row', split_axis=1, concat_axis=1, tiled=True)]
    all_to_all x1 -> x0, starting transfers between devices: 8.02 us -> none  [per_device(): lax.all_to_all(shaped, 'row', split_axis=1, concat_axis=1, tiled=True)]
  transfers between devices with their start and end apart: 3 -> 0, of which waited for: 3 -> 0; matrix products, arithmetic and copies ran while one was open for 0% -> 0% of each run, Pallas kernels for 0% -> 0%
where the time goes in v3:
time: 128 us
  Pallas kernels  127 us (99%)
    pallas_call x1, Pallas kernels, per_device(): pl.pallas_call(functools.partial(kernel, rows, depth), out_shape=pltpu.VM...  127 us

profile of v3, /device:TPU:1, one launch (start us, length us, event | category | flops | bytes accessed | tf_op | source)
XLA Modules:
  0.0 127.7 jit_solution(14095920451683087678)
XLA Ops:
  0.0 126.7 %ladder.1 = f32[1232,256]{1,0:T(8,128)S(1)} custom-call(f32[1232,2464]{1,0:T(8,128)} %v_hbm.1, f32[1232,256]{1,0:T(8,128)} %amp_hbm.1, s32[16]{0:T(128)} %phase.1), custom_call_target="tpu_custom_call" | custom-call | tf_op jit(solution)/shard_map/ladder/pallas_call | solution.py:422
  126.7 1.0 copy.5

commit v4 on v3

--- a/solution.py
+++ b/solution.py
@@ -7,7 +7,7 @@
 from jax.experimental.pallas import tpu as pltpu
 from jax.sharding import PartitionSpec as P
 
-UNITS = (("A", 1, 0), ("A", 0, 0), ("M", 1, 0), ("M", 1, 1), ("M", 0, 0), ("D", 1, 0), ("M", 0, 1), ("D", 0, 0))
+UNITS = (("A", 1, 0), ("A", 0, 0), ("M", 1, 0), ("M", 1, 1), ("D", 1, 0), ("M", 0, 0), ("M", 0, 1), ("D", 0, 0))
 N_UNITS = 8
 KPAD = 160
 KTOT = 16 * KPAD
@@ -16,7 +16,7 @@
 RT = 176
 CUT = 4
 STEPS = ((0, 0, KPAD // 2), (0, KPAD // 2, KPAD // 2)) + tuple((u, 0, KPAD) for u in range(1, N_UNITS))
-NO_Y2 = (0, 1, 8)
+NO_Y2 = (0, 1, 7, 8)
 CHUNKS = (((0, RT), (2 * RT, RT), (4 * RT, RT), (6 * RT, RT // 2)),
           ((RT, RT), (3 * RT, RT), (5 * RT, RT), (6 * RT + RT // 2, RT // 2)))
 MESH = pl.DeviceIdType.MESH
@@ -24,8 +24,7 @@
 
 def kernel(rows, depth, v_hbm, amp_hbm, phase, out,
            amp, apad, perm, T, Vh, Vl, Th, Tl, Pt, RA, RD, RY, Vs,
-           arecv, asend, yrecv, ysend, zrecv, zsend, frecv, fsend, drecv, dsend,
-           hrecv, hsend, xrecv, xsend, lrecv, lsend, vsem, asem):
+           arecv, yrecv, zrecv, frecv, drecv, hrecv, xrecv, lrecv, sent, vsem, asem):
     r = lax.axis_index("row")
     c = lax.axis_index("col")
     x = c // 2
@@ -54,6 +53,9 @@
             src_ref=src, dst_ref=dst, send_sem=ssem, recv_sem=rsem,
             device_id={"row": row, "col": col}, device_id_type=MESH)
 
+    a_copy = pltpu.make_async_copy(amp_hbm, amp, asem)
+    a_copy.start()
+
     barrier = pltpu.get_barrier_semaphore()
     peers = [(row_of(o), col_of(dx, o)) for dx in range(4) for o in (0, 1) if (dx, o) != (0, 0)]
     peers += [(row_y, c), (row_zp, c), (row_zm, c), (row_c, c), (r, col_of(0, 1))]
@@ -86,14 +88,13 @@
         dcol = col_of(4 - dx, o)
         return remote(apad.at[dcol, pl.ds(lo, n), pl.ds(c0, w)],
                       T.at[u, slot(z, yl), pl.ds(lo, n), pl.ds(d0, w)],
-                      asend.at[g, i], arecv.at[g, i], row_of(o), dcol)
-
-    def a2a_in(g, i):
-        u, lo, n = STEPS[g]
-        _, c0, w, d0 = a2a_parts(g)[i]
-        return remote(apad.at[0, pl.ds(lo, n), pl.ds(c0, w)],
-                      T.at[u, slot(z, own(u)), pl.ds(lo, n), pl.ds(d0, w)],
-                      asend.at[g, i], arecv.at[g, i], r, c)
+                      sent.at[0], arecv.at[g], row_of(o), dcol)
+
+    def arrival(ref, sem):
+        return remote(ref, ref, sent.at[0], sem, r, c)
+
+    def all_sent(ref, k):
+        remote(ref, ref, sent.at[k], sent.at[k], r, c).wait_send()
 
     def send_out(*gs):
         for g in gs:
@@ -102,19 +103,19 @@
 
     def ycopy(g, i):
         ref = piece(g, zs[3 * i], own(STEPS[g][0]))
-        return remote(ref, ref, ysend.at[g, i], yrecv.at[g, i], row_y, c)
+        return remote(ref, ref, sent.at[1], yrecv.at[g, i], row_y, c)
 
     def ycopy_in(g, i):
         ref = piece(g, zs[3 * i], 1 - own(STEPS[g][0]))
-        return remote(ref, ref, ysend.at[g, i], yrecv.at[g, i], row_y, c)
+        return remote(ref, ref, sent.at[1], yrecv.at[g, i], row_y, c)
 
     def zcopy(g, way, k):
         ref = piece(g, z, (own(STEPS[g][0]) + k) % 2)
-        return remote(ref, ref, zsend.at[g, way * 2 + k], zrecv.at[g, way * 2 + k], row_z[way], c)
+        return remote(ref, ref, sent.at[2], zrecv.at[g, way * 2 + k], row_z[way], c)
 
     def zcopy_in(g, way, k):
         ref = piece(g, zs[1 + way], (own(STEPS[g][0]) + k) % 2)
-        return remote(ref, ref, zsend.at[g, way * 2 + k], zrecv.at[g, way * 2 + k], row_z[way], c)
+        return remote(ref, ref, sent.at[2], zrecv.at[g, way * 2 + k], row_z[way], c)
 
     def fpart(g, way, zz, k):
         u, lo, n = STEPS[g]
@@ -122,11 +123,10 @@
 
     def fcopy(g, way, k=0):
         ref = fpart(g, way, zs[1 + way], k)
-        return remote(ref, ref, fsend.at[g, k * 2 + way], frecv.at[g, k * 2 + way], row_z[way], c)
-
-    def fcopy_in(g, way, k=0):
-        ref = fpart(g, way, zs[3], k)
-        return remote(ref, ref, fsend.at[g, k * 2 + way], frecv.at[g, k * 2 + way], row_z[way], c)
+        return remote(ref, ref, sent.at[3], frecv.at[g, k], row_z[way], c)
+
+    def fcopy_in(g, k=0):
+        return arrival(piece(g, zs[3], (own(STEPS[g][0]) + k) % 2), frecv.at[g, k])
 
     def dpair(g, i, k):
         u, lo, n = STEPS[g]
@@ -134,19 +134,18 @@
 
     def dcopy(g, i):
         ref = dpair(g, i, core)
-        return remote(ref, ref, dsend.at[g, i], drecv.at[g, i], row_c, c)
-
-    def dcopy_in(g, i):
-        ref = dpair(g, i, 1 - core)
-        return remote(ref, ref, dsend.at[g, i], drecv.at[g, i], row_c, c)
+        return remote(ref, ref, sent.at[4], drecv.at[g], row_c, c)
+
+    def dcopy_in(g):
+        u, lo, n = STEPS[g]
+        return arrival(T.at[u, pl.ds((1 - core) * 8, 8), pl.ds(lo, n)], drecv.at[g])
 
     def local(g):
         return UNITS[STEPS[g][0]][:2] == ("D", 0)
 
     def Y0(g):
         if not local(g):
-            for i in range(len(a2a_parts(g))):
-                a2a_in(g, i).wait_recv()
+            arrival(piece(g, z, own(STEPS[g][0])), arecv.at[g]).wait_recv()
         ycopy(g, 0).start()
 
     def Z0(g):
@@ -169,8 +168,7 @@
             fcopy(g, way).start()
 
     def E4(g):
-        fcopy_in(g, 0).wait_recv()
-        fcopy_in(g, 1).wait_recv()
+        fcopy_in(g).wait_recv()
         if g not in NO_Y2:
             ycopy(g, 1).start()
 
@@ -183,15 +181,13 @@
 
     def E6(g):
         if g in NO_Y2:
-            fcopy_in(g, 0, 1).wait_recv()
-            fcopy_in(g, 1, 1).wait_recv()
+            fcopy_in(g, 1).wait_recv()
         else:
             ycopy_in(g, 1).wait_recv()
         dcopy(g, 3).start()
 
     def E7(g):
-        for i in range(4):
-            dcopy_in(g, i).wait_recv()
+        dcopy_in(g).wait_recv()
 
     def vprep(lo, hi):
         @pl.loop(lo, hi)
@@ -271,18 +267,18 @@
     def half_copy(h, way, i):
         lo, n = CHUNKS[way][i]
         return remote(Pt.at[UNITS.index(("A", h, 0)), pl.ds(lo, n)], RA.at[h * 2 + way, pl.ds(i * RT, n)],
-                      hsend.at[h * 2 + way, i], hrecv.at[h * 2 + way, i], r, col_of((1, 3)[way], 0))
+                      sent.at[5], hrecv.at[h * 2 + way, i // 2], r, col_of((1, 3)[way], 0))
 
     def full_copy(h, way, p, k):
         lo, n = part(k)
         i = h * 2 + way
         return remote(Pt.at[UNITS.index(("M", h, p)), pl.ds(lo, n), pl.ds(way * HB, HB)],
                       RD.at[i, pl.ds(lo, n), pl.ds(p * HB, HB)],
-                      xsend.at[i, p * 2 + k], xrecv.at[i, p * 2 + k], r, col_of((1, 3)[way], 0))
+                      sent.at[6], xrecv.at[h, p], r, col_of((1, 3)[way], 0))
 
     def last_copy(p):
         cs = pl.ds(p * HB, HB)
-        return remote(Pt.at[UNITS.index(("D", 1, 0)), :, cs], RY.at[:, cs], lsend.at[p], lrecv.at[p],
+        return remote(Pt.at[UNITS.index(("D", 1, 0)), :, cs], RY.at[:, cs], sent.at[7], lrecv.at[p],
                       r, col_of(0, 1))
 
     def reduce_step(u, k):
@@ -293,18 +289,17 @@
                 half_copy(h, 1, i).start()
         elif kind == "M" and k > 0:
             for way in (0, 1):
+                if p == 0:
+                    rs = ((0, 2 * RT), (2 * RT, RT + RT // 2))[k - 1]
+                    arrival(RA.at[h * 2 + way, pl.ds(*rs)], hrecv.at[h * 2 + way, k - 1]).wait_recv()
                 for i in ((0, 1), (2, 3))[k - 1]:
-                    if p == 0:
-                        half_copy(h, way, i).wait_recv()
                     lo, n = CHUNKS[way][i]
                     add_at(Pt.at[u], RA.at[h * 2 + way], lo, n, i * RT - lo, way * HB, p * HB)
                 full_copy(h, way, p, k - 1).start()
 
     def finish(h, p):
         u = UNITS.index(("D", h, 0))
-        for k in (0, 1):
-            for way in (0, 1):
-                full_copy(h, way, p, k).wait_recv()
+        arrival(RD.at[pl.ds(h * 2, 2), :, pl.ds(p * HB, HB)], xrecv.at[h, p]).wait_recv()
         srcs = [RD.at[h * 2], RD.at[h * 2 + 1]]
         if h == 0:
             last_copy(p).wait_recv()
@@ -320,34 +315,38 @@
         mm(u, 0, 2)
         reduce_step(u, 0)
         if u == 0:
+            E3(2)
+            Z0(3)
             mm(u, 2, CUT)
             reduce_step(u, 1)
         if u + 1 < N_UNITS:
             E4(u + 2)
             E5(u + 2)
+        if u < 2:
+            E2(u + 3)
+            E3(u + 3)
         if u == 0:
-            E2(3)
-            E3(3)
             E1(4)
+            E1(5)
         else:
+            if u == 1:
+                E1(6)
             mm(u, 2, CUT)
             reduce_step(u, 1)
+        if u == 6:
+            finish(1, 1)
         mm(u, CUT, n_rt)
         reduce_step(u, 2)
-        if u == 5:
+        if u == 4:
             finish(1, 0)
-        if u == 6:
-            finish(1, 1)
         if u + 1 < N_UNITS:
             E6(u + 2)
-        if u + 3 < N_UNITS:
+        if 0 < u < N_UNITS - 3:
             E2(u + 4)
             E3(u + 4)
-        if u + 4 < N_UNITS:
-            E1(u + 5)
-
-    a_copy = pltpu.make_async_copy(amp_hbm, amp, asem)
-    a_copy.start()
+        if 0 < u < N_UNITS - 5:
+            E1(u + 6)
+
     v_copy(0, 0).start()
     permprep()
     a_copy.wait()
@@ -382,37 +381,18 @@
     prep(0)
     E7(1)
     prep(1)
-    E3(2)
-    Z0(3)
     for u in range(N_UNITS):
         unit(u)
     finish(0, 0)
-    for g in range(len(STEPS)):
-        if not local(g):
-            for i in range(len(a2a_parts(g))):
-                a2a(g, i).wait_send()
-        for i in (0, 1):
-            if i == 0 or g not in NO_Y2:
-                ycopy(g, i).wait_send()
-            fcopy(g, i).wait_send()
-            if g in NO_Y2:
-                fcopy(g, i, 1).wait_send()
-            for k in (0, 1):
-                zcopy(g, i, k).wait_send()
-        for i in range(4):
-            dcopy(g, i).wait_send()
-    for h in (1, 0):
-        for way in (0, 1):
-            for i in range(4):
-                half_copy(h, way, i).wait_send()
-                if h == 1 or i < 2:
-                    full_copy(h, way, i // 2, i % 2).wait_send()
-    last_copy(0).wait_send()
+    all_sent(T.at[0, 0:7], 0)
+    all_sent(T.at[0, 0:2 * 8 - len(set(STEPS[g][0] for g in NO_Y2))], 1)
+    all_sent(T.at[0:2], 2)
+    all_sent(T.at[0, 0:8 + len(set(STEPS[g][0] for g in NO_Y2))], 3)
+    all_sent(T.at[0:4], 4)
+    all_sent(Pt.at[0:2], 5)
     finish(0, 1)
-    last_copy(1).wait_send()
-    for way in (0, 1):
-        for k in (0, 1):
-            full_copy(0, way, 1, k).wait_send()
+    all_sent(Pt.at[0:4], 6)
+    all_sent(RY, 7)
 
 
 def per_device(ladder_ints, amplitudes, phase_map):
@@ -439,9 +419,8 @@
             pltpu.VMEM((4, rows, NB), f32),
             pltpu.VMEM((rows, NB), f32),
             pltpu.VMEM((2, RT, depth), f32),
-            dma((9, 2)), dma((9, 2)), dma((9, 2)), dma((9, 2)), dma((9, 4)), dma((9, 4)), dma((9, 4)), dma((9, 4)),
-            dma((9, 4)), dma((9, 4)), dma((4, 4)), dma((4, 4)), dma((4, 4)), dma((4, 4)), dma((2,)), dma((2,)),
-            dma((2,)), dma,
+            dma((9,)), dma((9, 2)), dma((9, 4)), dma((9, 2)), dma((9,)), dma((4, 2)), dma((2, 2)), dma((2,)),
+            dma((8,)), dma((2,)), dma,
         ],
         compiler_params=pltpu.CompilerParams(
             collective_id=0, has_side_effects=True, vmem_limit_bytes=65600000),

time: 128 us -> 121 us (0.945)
  Pallas kernels: 127 us -> 120 us
    pallas_call x1, Pallas kernels: 127 us -> 120 us  [per_device(): pl.pallas_call(functools.partial(kernel, rows, depth), out_shape=pltpu.VM...]
where the time goes in v4:
time: 121 us
  Pallas kernels  120 us (99%)
    pallas_call x1, Pallas kernels, per_device(): pl.pallas_call(functools.partial(kernel, rows, depth), out_shape=pltpu.VM...  120 us

profile of v4, /device:TPU:1, one launch (start us, length us, event | category | flops | bytes accessed | tf_op | source)
XLA Modules:
  0.0 120.8 jit_solution(10437523289500998642)
XLA Ops:
  0.0 119.7 %ladder.1 = f32[1232,256]{1,0:T(8,128)S(1)} custom-call(f32[1232,2464]{1,0:T(8,128)} %v_hbm.1, f32[1232,256]{1,0:T(8,128)} %amp_hbm.1, s32[16]{0:T(128)} %phase.1), custom_call_target="tpu_custom_call" | custom-call | tf_op jit(solution)/shard_map/ladder/pallas_call | solution.py:402
  119.7 1.0 copy.5

commit v5 on v4

--- a/solution.py
+++ b/solution.py
@@ -17,8 +17,7 @@
 CUT = 4
 STEPS = ((0, 0, KPAD // 2), (0, KPAD // 2, KPAD // 2)) + tuple((u, 0, KPAD) for u in range(1, N_UNITS))
 NO_Y2 = (0, 1, 7, 8)
-CHUNKS = (((0, RT), (2 * RT, RT), (4 * RT, RT), (6 * RT, RT // 2)),
-          ((RT, RT), (3 * RT, RT), (5 * RT, RT), (6 * RT + RT // 2, RT // 2)))
+RH = RT // 2
 MESH = pl.DeviceIdType.MESH
 
 
@@ -244,6 +243,9 @@
             acc += jnp.dot(Vl[rs, :], Th[...], preferred_element_type=jnp.float32)
             acc += jnp.dot(vh, Th[...], preferred_element_type=jnp.float32)
             Pt[u, rs, :] = acc
+            if UNITS[u][0] == "A":
+                half_copy(UNITS[u][1], 0, i).start()
+                half_copy(UNITS[u][1], 1, i).start()
 
     def add_at(dst, src, lo, n, off, d0, s0):
         @pl.loop(0, n // 88)
@@ -265,9 +267,9 @@
         return (0, cut) if k == 0 else (cut, rows - cut)
 
     def half_copy(h, way, i):
-        lo, n = CHUNKS[way][i]
-        return remote(Pt.at[UNITS.index(("A", h, 0)), pl.ds(lo, n)], RA.at[h * 2 + way, pl.ds(i * RT, n)],
-                      sent.at[5], hrecv.at[h * 2 + way, i // 2], r, col_of((1, 3)[way], 0))
+        return remote(Pt.at[UNITS.index(("A", h, 0)), pl.ds(i * RT + way * RH, RH)],
+                      RA.at[h * 2 + way, pl.ds(i * RH, RH)],
+                      sent.at[5], hrecv.at[h * 2 + way, i // CUT], r, col_of((1, 3)[way], 0))
 
     def full_copy(h, way, p, k):
         lo, n = part(k)
@@ -283,19 +285,15 @@
 
     def reduce_step(u, k):
         kind, h, p = UNITS[u]
-        if kind == "A":
-            for i in ((0,), (1,), (2, 3))[k]:
-                half_copy(h, 0, i).start()
-                half_copy(h, 1, i).start()
-        elif kind == "M" and k > 0:
+        if kind == "M":
+            lo, hi = ((0, CUT), (CUT, n_rt))[k]
             for way in (0, 1):
                 if p == 0:
-                    rs = ((0, 2 * RT), (2 * RT, RT + RT // 2))[k - 1]
-                    arrival(RA.at[h * 2 + way, pl.ds(*rs)], hrecv.at[h * 2 + way, k - 1]).wait_recv()
-                for i in ((0, 1), (2, 3))[k - 1]:
-                    lo, n = CHUNKS[way][i]
-                    add_at(Pt.at[u], RA.at[h * 2 + way], lo, n, i * RT - lo, way * HB, p * HB)
-                full_copy(h, way, p, k - 1).start()
+                    arrival(RA.at[h * 2 + way, pl.ds(lo * RH, (hi - lo) * RH)], hrecv.at[h * 2 + way, k]).wait_recv()
+                for i in range(lo, hi):
+                    first = i * RT + way * RH
+                    add_at(Pt.at[u], RA.at[h * 2 + way], first, RH, i * RH - first, way * HB, p * HB)
+                full_copy(h, way, p, k).start()
 
     def finish(h, p):
         u = UNITS.index(("D", h, 0))
@@ -313,49 +311,52 @@
             E7(u + 1)
             prep(u + 1)
         mm(u, 0, 2)
-        reduce_step(u, 0)
         if u == 0:
             E3(2)
             Z0(3)
             mm(u, 2, CUT)
-            reduce_step(u, 1)
+            E4(2)
+            E5(2)
+            E2(3)
+            mm(u, CUT, n_rt)
+            E3(3)
+            E1(4)
+            E1(5)
+            E6(2)
+            return
         if u + 1 < N_UNITS:
             E4(u + 2)
             E5(u + 2)
-        if u < 2:
-            E2(u + 3)
-            E3(u + 3)
-        if u == 0:
-            E1(4)
-            E1(5)
-        else:
-            if u == 1:
-                E1(6)
-            mm(u, 2, CUT)
-            reduce_step(u, 1)
+        if u == 1:
+            E2(4)
+            E3(4)
+            E1(6)
+        mm(u, 2, CUT)
+        reduce_step(u, 0)
         if u == 6:
             finish(1, 1)
         mm(u, CUT, n_rt)
-        reduce_step(u, 2)
+        reduce_step(u, 1)
         if u == 4:
             finish(1, 0)
         if u + 1 < N_UNITS:
             E6(u + 2)
-        if 0 < u < N_UNITS - 3:
+        if u < N_UNITS - 3:
             E2(u + 4)
             E3(u + 4)
-        if 0 < u < N_UNITS - 5:
+        if u < N_UNITS - 6:
             E1(u + 6)
 
     v_copy(0, 0).start()
     permprep()
     a_copy.wait()
     aprep()
+    T[N_UNITS - 1, slot(z, yl)] = apad[c]
     pl.semaphore_wait(barrier, len(peers))
     send_out(0, 1)
+    E1(8)
     vprep(0, 3)
     send_out(2, 3, 4)
-    T[N_UNITS - 1, slot(z, yl)] = apad[c]
     vprep(3, 4)
     E1(0)
     send_out(5, 6, 7)
@@ -385,9 +386,12 @@
         unit(u)
     finish(0, 0)
     all_sent(T.at[0, 0:7], 0)
-    all_sent(T.at[0, 0:2 * 8 - len(set(STEPS[g][0] for g in NO_Y2))], 1)
+    over_z = sum(STEPS[g][2] for g in NO_Y2)
+    for rows_sent, k in ((16 * KPAD - over_z, 1), (8 * KPAD + over_z, 3)):
+        all_sent(T.at[0, 0:rows_sent // KPAD], k)
+        if rows_sent % KPAD:
+            all_sent(T.at[0, 0, 0:rows_sent % KPAD], k)
     all_sent(T.at[0:2], 2)
-    all_sent(T.at[0, 0:8 + len(set(STEPS[g][0] for g in NO_Y2))], 3)
     all_sent(T.at[0:4], 4)
     all_sent(Pt.at[0:2], 5)
     finish(0, 1)

time: 121 us -> 119 us (0.983)
  Pallas kernels: 120 us -> 118 us
    pallas_call x1, Pallas kernels: 120 us -> 118 us  [per_device(): pl.pallas_call(functools.partial(kernel, rows, depth), out_shape=pltpu.VM...]
where the time goes in v5:
time: 119 us
  Pallas kernels  118 us (99%)
    pallas_call x1, Pallas kernels, per_device(): pl.pallas_call(functools.partial(kernel, rows, depth), out_shape=pltpu.VM...  118 us

profile of v5, /device:TPU:1, one launch (start us, length us, event | category | flops | bytes accessed | tf_op | source)
XLA Modules:
  0.0 118.6 jit_solution(8273053400063354680)
XLA Ops:
  0.0 117.6 %ladder.1 = f32[1232,256]{1,0:T(8,128)S(1)} custom-call(f32[1232,2464]{1,0:T(8,128)} %v_hbm.1, f32[1232,256]{1,0:T(8,128)} %amp_hbm.1, s32[16]{0:T(128)} %phase.1), custom_call_target="tpu_custom_call" | custom-call | tf_op jit(solution)/shard_map/ladder/pallas_call | solution.py:406
  117.6 1.0 copy.5

commit v6 on v5

--- a/solution.py
+++ b/solution.py
@@ -364,8 +364,8 @@
     E1(1)
     vprep(5, 6)
     E2(0)
+    E2(1)
     E3(0)
-    E2(1)
     E3(1)
     Y0(2)
     vprep(6, 7)

time: 119 us -> 118 us (level)
  Pallas kernels: 118 us -> 116 us
where the time goes in v6:
time: 118 us; the launch traced here: 117 us
  Pallas kernels  116 us (98%)
    pallas_call x1, Pallas kernels, per_device(): pl.pallas_call(functools.partial(kernel, rows, depth), out_shape=pltpu.VM...  116 us

profile of v6, /device:TPU:1, one launch (start us, length us, event | category | flops | bytes accessed | tf_op | source)
XLA Modules:
  0.0 117.5 jit_solution(6586657079563624522)
XLA Ops:
  0.0 116.4 %ladder.1 = f32[1232,256]{1,0:T(8,128)S(1)} custom-call(f32[1232,2464]{1,0:T(8,128)} %v_hbm.1, f32[1232,256]{1,0:T(8,128)} %amp_hbm.1, s32[16]{0:T(128)} %phase.1), custom_call_target="tpu_custom_call" | custom-call | tf_op jit(solution)/shard_map/ladder/pallas_call | solution.py:406
  116.4 1.0 copy.5
